TPU v7x, 32 devices: a whole 2x2x4 slice. The times are simulated.
32 devices in a mesh: dp: 4 (over y, x), tensor: 8 (over z, core).
Axes of the slice: x: 2, y: 2, z: 4, core: 2. Of those that a mesh axis runs over, the one named last changes fastest.
Arguments:
- tokens: bfloat16 [2048, 4096], P(('dp', 'tensor')), parts along dimension 0, may hold values from -6 to 6
- norm_gain: float32 [4096], replicated, may hold values from 0.5 to 1.5
- gate_weight: bfloat16 [4096, 14336], P(None, 'tensor'), may hold values from -0.09375 to 0.09375
- up_weight: bfloat16 [4096, 14336], P(None, 'tensor'), may hold values from -0.09375 to 0.09375
- down_weight: bfloat16 [14336, 4096], P('tensor'), may hold values from -0.0625 to 0.0625
Outputs:
- mixed: bfloat16 [2048, 4096], P('dp', 'tensor'), parts along dimension 0
There are 4 independent parts, one for each index of `dp`. A program takes and returns all parts, laid end to end along the dimension named above; an argument that names none is the same for every part. Nothing has to cross between parts.
All inputs are finite; a program needn't handle non-finite values.
Results may differ from a plain program's by a relative error of at most 0.0053.
Values may be sent and summed in bfloat16 or wider, within the bound.
A program may use at most 128 MiB of HBM per device.

v0:
```python
import jax
import jax.numpy as jnp
from jax import lax
from jax.sharding import PartitionSpec as P


def on_device(tokens, norm_gain, gate_weight, up_weight, down_weight):
    wide = tokens.astype(jnp.float32)
    square_mean = jnp.mean(wide * wide, axis=1, keepdims=True)
    normed = (wide * norm_gain[None, :] / jnp.sqrt(square_mean + 1e-05)).astype(jnp.bfloat16)
    piece = lax.all_gather(normed, "tensor", axis=0, tiled=True)
    gate = jnp.dot(piece, gate_weight, preferred_element_type=jnp.float32)
    up = jnp.dot(piece, up_weight, preferred_element_type=jnp.float32)
    hidden = (jax.nn.silu(gate) * up).astype(jnp.bfloat16)
    residual = lax.all_to_all(tokens, "tensor", split_axis=1, concat_axis=0, tiled=True)
    summed = lax.psum_scatter(
        jnp.einsum("fc,tf->ct", down_weight, hidden, preferred_element_type=jnp.float32),
        "tensor",
        scatter_dimension=0,
        tiled=True,
    )
    return (residual.astype(jnp.float32) + summed.T).astype(jnp.bfloat16)


def solution(mesh):
    return jax.shard_map(
        on_device,
        mesh=mesh,
        in_specs=(
            P(("dp", "tensor"), None),
            P(),
            P(None, "tensor"),
            P(None, "tensor"),
            P("tensor", None),
        ),
        out_specs=P("dp", "tensor"),
        check_vma=False,
    )
```

profile of v0, /device:TPU:0, one launch (start us, length us, event | category | flops | bytes accessed | tf_op | source)
XLA Modules:
  0.0 211.6 jit_solution(6932969058489958926)
XLA Ops:
  6.5 0.0 all-gather.2.cloned.1.call-start
  6.5 1.2 fusion.3
  7.8 2.0 fusion.2
  9.8 0.0 all-gather.2.cloned.1.call-update
  9.8 0.0 reduce-scatter.2.cloned.1.call-start
  9.9 49.7 %all-gather.2.cloned.1.call-done = bf16[512,4096]{1,0:T(8,128)(2,1)} async-done(((bf16[64,4096]{1,0:T(8,128)(2,1)}), bf16[512,4096]{1,0:T(8,128)(2,1)}) %all-gather.2.cloned.1.call-update) | async-done | bytes 4194320 | tf_op jit(solution)/shard_map/all_gather | solution.py:11
  59.6 14.8 %fusion.6 = f32[512,1792]{1,0:T(8,128)} fusion(bf16[512,4096]{1,0:T(8,128)(2,1)} %all-gather.2.cloned.1.call-done, bf16[4096,1792]{1,0:T(8,128)(2,1)} %param.7), kind=kOutput, calls=%fused_computation.13 | convolution fusion | flops 7516192768 | bytes 22544384 | tf_op jit(solution)/shard_map/dot_general | solution.py:12
  74.4 31.2 %convolution_bitcast_fusion = f32[4096,512]{0,1:T(8,128)} fusion(bf16[1792,4096]{1,0:T(8,128)(2,1)} %param.9, f32[512,1792]{1,0:T(8,128)} %fusion.6, bf16[512,4096]{1,0:T(8,128)(2,1)} %all-gather.2.cloned.1.call-done, bf16[4096,1792]{1,0:T(8,128)(2,1)} %param.8), kind=kOutput, calls=%fused_computation | convolution fusion | flops 15037890560 | bytes 45613056 | tf_op jit(solution)/shard_map/fc,tf->ct/dot_general | solution.py:17
  105.6 0.0 copy-start
  105.6 0.0 reduce-scatter.2.cloned.1.call-update
  105.6 1.0 copy-done
  106.7 25.3 %all_to_all.13 = bf16[64,8,512]{2,0,1:T(8,128)(2,1)S(1)} all-to-all(bf16[64,8,512]{2,0,1:T(8,128)(2,1)S(1)} %bitcast.20), channel_id=1, replica_groups=mesh['dp'=4,'tensor'=8] {'tensor'}, dimensions={1} | all-to-all | bytes 1048576 | tf_op jit(solution)/shard_map/all_to_all | solution.py:15
  132.0 70.6 %reduce-scatter.2.cloned.1.call-done = f32[512,512]{0,1:T(8,128)} async-done(((f32[4096,512]{0,1:T(8,128)}), f32[512,512]{0,1:T(8,128)}) %reduce-scatter.2.cloned.1.call-update) | async-done | bytes 1048592 | tf_op jit(solution)/shard_map/reduce_scatter | solution.py:16
  202.6 2.2 %fusion.4 = bf16[512,512]{1,0:T(8,128)(2,1)} fusion(f32[512,512]{0,1:T(8,128)} %reduce-scatter.2.cloned.1.call-done, bf16[64,8,512]{2,0,1:T(8,128)(2,1)S(1)} %all_to_all.13), kind=kLoop, calls=%fused_computation.9 | loop fusion | flops 786432 | bytes 2097152 | tf_op jit(solution)/shard_map/convert_element_type | solution.py:22
  (2 shorter events, 0.0 us)
Async XLA Ops:
  6.5 53.0 %all-gather.2.cloned.1.call-start = ((), (), s32[]{:S(2)}) async-start(), calls=%async_computation.2 | async-start | bytes 4718592 | tf_op jit(solution)/shard_map/all_gather | solution.py:11
  9.8 192.7 %reduce-scatter.2.cloned.1.call-start = ((), (), s32[]{:S(2)}) async-start(), calls=%async_computation.3 | async-start | bytes 9437184 | tf_op jit(solution)/shard_map/reduce_scatter | solution.py:16
  105.6 1.0 copy-start
Sparse Core Ops, SparseCore 0:
  9.9 49.5 all-gather.1
  105.7 96.7 reduce-scatter.1
where the time goes:
time: 212 us
  waiting for transfers between devices  120 us (57%)
  matrix products  46 us (22%)
  blocking collectives  25.3 us (12%)
  between operations  13.4 us (6%)
  other arithmetic  5.41 us (3%)
    reduce_scatter x1, waiting for transfers between devices, on_device(): lax.psum_scatter(jnp.einsum('fc,tf->ct', down_weight, hidden, preferred_e...  70.6 us
    all_gather x1, waiting for transfers between devices, on_device(): piece = lax.all_gather(normed, 'tensor', axis=0, tiled=True)  49.7 us
    dot_general x1, matrix products, on_device(): jnp.einsum('fc,tf->ct', down_weight, hidden, preferred_element_type=jnp.f...  31.2 us
    all_to_all x1, blocking collectives, on_device(): lax.all_to_all(tokens, 'tensor', split_axis=1, concat_axis=0, tiled=True)  25.3 us
    dot_general x1, matrix products, on_device(): gate = jnp.dot(piece, gate_weight, preferred_element_type=jnp.float32)  14.8 us
  transfers between devices with their start and end apart: 2, of which 2 were waited for; matrix products, arithmetic and copies ran while one was open for 0% of the time, Pallas kernels for 0%

commit v1 on v0

v1 whole, which is shorter than its diff:
```python
import jax
import jax.numpy as jnp
from jax import lax
from jax.sharding import PartitionSpec as P


def on_device(tokens, norm_gain, gate_weight, up_weight, down_weight):
    n = lax.axis_size("tensor")
    me = lax.axis_index("tensor")
    every = lax.all_gather(tokens, "tensor", axis=0, tiled=True)
    wide = every.astype(jnp.float32)
    square_mean = jnp.mean(wide * wide, axis=1, keepdims=True)
    piece = (wide * norm_gain[None, :] / jnp.sqrt(square_mean + 1e-05)).astype(jnp.bfloat16)
    gate = jnp.dot(piece, gate_weight, preferred_element_type=jnp.float32)
    up = jnp.dot(piece, up_weight, preferred_element_type=jnp.float32)
    hidden = (jax.nn.silu(gate) * up).astype(jnp.bfloat16)
    width = every.shape[1] // n
    residual = lax.dynamic_slice_in_dim(every, me * width, width, axis=1)
    summed = lax.psum_scatter(
        jnp.einsum("fc,tf->ct", down_weight, hidden, preferred_element_type=jnp.float32).astype(jnp.bfloat16),
        "tensor",
        scatter_dimension=0,
        tiled=True,
    )
    return (residual.astype(jnp.float32) + summed.T.astype(jnp.float32)).astype(jnp.bfloat16)


def solution(mesh):
    return jax.shard_map(
        on_device,
        mesh=mesh,
        in_specs=(
            P(("dp", "tensor"), None),
            P(),
            P(None, "tensor"),
            P(None, "tensor"),
            P("tensor", None),
        ),
        out_specs=P("dp", "tensor"),
        check_vma=False,
    )
```

time: 212 us -> 162 us (0.76)
  blocking collectives: 25.3 us -> 0 us
  waiting for transfers between devices: 120 us -> 101 us
  matrix products: 46 us -> 42.4 us
    all_to_all x1 -> x0, blocking collectives: 25.3 us -> none  [on_device(): lax.all_to_all(tokens, 'tensor', split_axis=1, concat_axis=0, tiled=True)]
    reduce_scatter x1, waiting for transfers between devices: 70.6 us -> 48.9 us  [on_device(): lax.psum_scatter(jnp.einsum('fc,tf->ct', down_weight, hidden, preferred_e...]
    dot_general x1, matrix products: 31.2 us -> 28.8 us  [on_device(): jnp.einsum('fc,tf->ct', down_weight, hidden, preferred_element_type=jnp.f...]
where the time goes in v1:
time: 162 us
  waiting for transfers between devices  101 us (62%)
  matrix products  42.4 us (26%)
  between operations  13.4 us (8%)
  other arithmetic  5.37 us (3%)
    all_gather x1, waiting for transfers between devices, on_device(): every = lax.all_gather(tokens, 'tensor', axis=0, tiled=True)  51.3 us
    reduce_scatter x1, waiting for transfers between devices, on_device(): lax.psum_scatter(jnp.einsum('fc,tf->ct', down_weight, hidden, preferred_e...  48.9 us
    dot_general x1, matrix products, on_device(): jnp.einsum('fc,tf->ct', down_weight, hidden, preferred_element_type=jnp.f...  28.8 us
    dot_general x1, matrix products, on_device(): gate = jnp.dot(piece, gate_weight, preferred_element_type=jnp.float32)  13.6 us
  transfers between devices with their start and end apart: 2, of which 2 were waited for; matrix products, arithmetic and copies ran while one was open for 0% of the time, Pallas kernels for 0%

profile of v1, /device:TPU:0, one launch (start us, length us, event | category | flops | bytes accessed | tf_op | source)
XLA Modules:
  0.0 162.3 jit_solution(9622522727778714779)
XLA Ops:
  6.5 0.0 copy-start.1
  6.5 0.0 all-gather.2.cloned.1.call-start
  6.5 0.7 all-gather.2.cloned.1.call-update
  7.3 0.0 reduce-scatter.2.cloned.1.call-start
  7.3 51.3 %all-gather.2.cloned.1.call-done = bf16[512,4096]{1,0:T(8,128)(2,1)} async-done(((bf16[64,4096]{1,0:T(8,128)(2,1)}), bf16[512,4096]{1,0:T(8,128)(2,1)}) %all-gather.2.cloned.1.call-update) | async-done | bytes 4194320 | tf_op jit(solution)/shard_map/all_gather | solution.py:10
  58.6 0.0 copy-start
  58.6 3.2 %fusion.2 = f32[512]{0:T(512)S(1)} fusion(bf16[512,4096]{1,0:T(8,128)(2,1)} %all-gather.2.cloned.1.call-done), kind=kLoop, calls=%fused_computation.4 | loop fusion | flops 6290944 | bytes 4196352 | tf_op jit(solution)/shard_map/reduce_sum | solution.py:12
  61.8 0.0 copy-done.1
  61.8 0.2 copy-done
  62.0 13.6 %fusion.9 = f32[512,1792]{1,0:T(8,128)} fusion(bf16[4096,1792]{1,0:T(8,128)(2,1)} %param.7, bf16[512,4096]{1,0:T(8,128)(2,1)S(1)} %copy-done, f32[512]{0:T(512)S(1)} %add_sqrt_fusion, f32[4096]{0:T(1024)S(1)} %copy-done.1), kind=kOutput, calls=%fused_computation.13 | convolution fusion | flops 7524581376 | bytes 22562816 | tf_op jit(solution)/shard_map/dot_general | solution.py:14
  75.6 28.8 %fusion.3 = bf16[4096,512]{0,1:T(8,128)(2,1)} fusion(bf16[1792,4096]{1,0:T(8,128)(2,1)} %param.9, f32[512,1792]{1,0:T(8,128)} %fusion.9, bf16[4096,1792]{1,0:T(8,128)(2,1)} %param.8, bf16[512,4096]{1,0:T(8,128)(2,1)} %all-gather.2.cloned.1.call-done, f32[512]{0:T(512)S(1)} %add_sqrt_fusion, f32[4096]{0:T(1024)S(1)} %copy-done.1), kind=kOutput, calls=%fused_computation.6 | convolution fusion | flops 15048376320 | bytes 41437184 | tf_op jit(solution)/shard_map/fc,tf->ct/dot_general | solution.py:20
  104.4 0.0 reduce-scatter.2.cloned.1.call-update
  104.4 48.9 %reduce-scatter.2.cloned.1.call-done = bf16[512,512]{0,1:T(8,128)(2,1)} async-done(((bf16[4096,512]{0,1:T(8,128)(2,1)}), bf16[512,512]{0,1:T(8,128)(2,1)}) %reduce-scatter.2.cloned.1.call-update) | async-done | bytes 524304 | tf_op jit(solution)/shard_map/reduce_scatter | solution.py:19
  153.3 2.1 %fusion.5 = bf16[512,512]{1,0:T(8,128)(2,1)} fusion(bf16[512,512]{0,1:T(8,128)(2,1)} %reduce-scatter.2.cloned.1.call-done, bf16[512,4096]{1,0:T(8,128)(2,1)} %all-gather.2.cloned.1.call-done, s32[]{:T(128)S(6)} %select_n.3), kind=kLoop, calls=%fused_computation.10 | loop fusion | flops 1048576 | bytes 1572868 | tf_op jit(solution)/shard_map/convert_element_type | solution.py:25
  (1 shorter events, 0.0 us)
Async XLA Ops:
  6.5 55.3 %copy-start.1 = (f32[4096]{0:T(1024)S(1)}, f32[4096]{0:T(1024)}, u32[]{:S(2)}) copy-start(f32[4096]{0:T(1024)} %param.6) | copy-start | bytes 49156
  6.5 52.0 %all-gather.2.cloned.1.call-start = ((), (), s32[]{:S(2)}) async-start(), calls=%async_computation.1 | async-start | bytes 4718592 | tf_op jit(solution)/shard_map/all_gather | solution.py:10
  7.3 146.1 %reduce-scatter.2.cloned.1.call-start = ((), (), s32[]{:S(2)}) async-start(), calls=%async_computation.2 | async-start | bytes 4718592 | tf_op jit(solution)/shard_map/reduce_scatter | solution.py:19
  58.6 3.4 %copy-start = (bf16[512,4096]{1,0:T(8,128)(2,1)S(1)}, bf16[512,4096]{1,0:T(8,128)(2,1)}, u32[]{:S(2)}) copy-start(bf16[512,4096]{1,0:T(8,128)(2,1)} %all-gather.2.cloned.1.call-done) | copy-start | bytes 12582916
Sparse Core Ops, SparseCore 0:
  8.9 49.5 all-gather.1
  104.6 48.7 reduce-scatter.1

commit v2 on v0

v2 whole, which is shorter than its diff:
```python
import functools

import jax
import jax.numpy as jnp
from jax import lax
from jax.experimental import pallas as pl
from jax.experimental.pallas import tpu as pltpu
from jax.sharding import PartitionSpec as P

HALVES = 2
VMEM_LIMIT = 67043328


def block_kernel(
    n, tok, gain, gw, uw, dw, out,
    gwv, uwv, dwv, every, normed, hidden, part, peer, arrived, acc,
    load_sem, own_sem, ag_recv, ag_send, peer_send, peer_recv, rs_send, rs_recv,
):
    H = HALVES
    dp = lax.axis_index("dp")
    me = lax.axis_index("tensor")
    C = n // 2
    p, c = me // 2, me % 2
    rows, D = tok.shape
    r = rows // H
    T = n * r
    F = gwv.shape[1]
    width = D // n
    partner = (dp, 2 * p + (1 - c))
    right = (dp, lax.rem(me + 2, n))
    left = (dp, lax.rem(me + n - 2, n))
    has_right, has_left = p < C - 1, p > 0

    loads = [pltpu.make_async_copy(a, b, load_sem.at[k]) for k, (a, b) in enumerate(((gw, gwv), (uw, uwv), (dw, dwv)))]

    def block(h, t):
        return every.at[h, pl.ds(pl.multiple_of(t * r, r), r), :]

    own = [pltpu.make_async_copy(tok.at[pl.ds(h * r, r), :], block(h, me), own_sem.at[h]) for h in range(H)]
    for copy in own:
        copy.start()
    for copy in loads:
        copy.start()

    barrier = pltpu.get_barrier_semaphore()

    def greet(device):
        pl.semaphore_signal(barrier, inc=1, device_id=device, device_id_type=pl.DeviceIdType.MESH)

    greet(partner)
    pl.when(has_right)(lambda: greet(right))
    pl.when(has_left)(lambda: greet(left))
    pl.semaphore_wait(barrier, 1 + has_right.astype(jnp.int32) + has_left.astype(jnp.int32))

    def remote(src, dst, s, d, device):
        return pltpu.make_async_remote_copy(
            src_ref=src, dst_ref=dst, send_sem=s, recv_sem=d, device_id=device, device_id_type=pl.DeviceIdType.MESH
        )

    def gather(h, t, way):
        return remote(block(h, t), block(h, t), ag_send.at[way, h, t], ag_recv.at[h, t], (right, left, partner)[way])

    def gather_first(h):
        own[h].wait()
        pl.when(has_right)(lambda: gather(h, me, 0).start())
        pl.when(has_left)(lambda: gather(h, me, 1).start())
        gather(h, me, 2).start()

    def gather_step(h, s):
        @pl.when(p - s >= 0)
        def _():
            t = me - 2 * s
            gather(h, t, 2).wait_recv()
            pl.when(has_right)(lambda: gather(h, t, 0).start())
            gather(h, t, 2).start()

        @pl.when(p + s <= C - 1)
        def _():
            t = me + 2 * s
            gather(h, t, 2).wait_recv()
            pl.when(has_left)(lambda: gather(h, t, 1).start())
            gather(h, t, 2).start()

    def gather_last(h):
        for q in range(C):
            gather(h, 2 * q + (1 - c), 2).wait_recv()

    def gather_drain(h):
        for q in range(C):
            t = 2 * q + c
            pl.when((q <= p) & has_right)(lambda: gather(h, t, 0).wait_send())
            pl.when((q >= p) & has_left)(lambda: gather(h, t, 1).wait_send())
            gather(h, t, 2).wait_send()

    def to_peer(h, q):
        return remote(part.at[h, 2 * q + (1 - c)], peer.at[h, q], peer_send.at[h, q], peer_recv.at[h, q], partner)

    def to_right(h, q):
        return remote(part.at[h, 2 * q + c], arrived.at[h, q], rs_send.at[h, q], rs_recv.at[h, q], right)

    def to_left(h, q):
        slot = jnp.where(q == p - 1, C, q)
        return remote(part.at[h, 2 * q + c], arrived.at[h, slot], rs_send.at[h, q], rs_recv.at[h, slot], left)

    def landed(h, slot):
        remote(arrived.at[h, slot], arrived.at[h, slot], rs_send.at[h, 0], rs_recv.at[h, slot], partner).wait_recv()

    def scatter_first(h):
        for q in range(C):
            to_peer(h, q).wait_recv()
            t = 2 * q + c
            part[h, t] = (part[h, t].astype(jnp.float32) + peer[h, q].astype(jnp.float32)).astype(jnp.bfloat16)

        @pl.when(p == 0)
        def _():
            for q in reversed(range(1, C)):
                to_right(h, q).start()

        @pl.when(p == C - 1)
        def _():
            for q in range(C - 1):
                to_left(h, q).start()

    def add_arrived(h, q):
        landed(h, q)
        t = 2 * q + c
        part[h, t] = (part[h, t].astype(jnp.float32) + arrived[h, q].astype(jnp.float32)).astype(jnp.bfloat16)

    def scatter_step(h, j):
        def rightward():
            q = C - 1 - j

            @pl.when((q > p) & has_left)
            def _():
                add_arrived(h, q)
                to_right(h, q).start()

        def leftward():
            @pl.when((j < p) & has_right)
            def _():
                add_arrived(h, j)
                to_left(h, j).start()

        @pl.when(2 * p < C)
        def _():
            rightward()
            leftward()

        @pl.when(2 * p >= C)
        def _():
            leftward()
            rightward()

    def scatter_last(h):
        lanes = pl.ds(pl.multiple_of(me * width, width), width)
        acc[...] = every[h, :, lanes].astype(jnp.float32) + part[h, me].astype(jnp.float32)

        @pl.when(has_left)
        def _():
            landed(h, p)
            acc[...] += arrived[h, p].astype(jnp.float32)

        @pl.when(has_right)
        def _():
            landed(h, C)
            acc[...] += arrived[h, C].astype(jnp.float32)

        for t in range(n):
            out[t * rows + h * r : t * rows + (h + 1) * r, :] = acc[t * r : (t + 1) * r, :].astype(jnp.bfloat16)

    def scatter_drain(h):
        for q in range(C):
            to_peer(h, q).wait_send()
            pl.when(q > p)(lambda: to_right(h, q).wait_send())
            pl.when(q < p)(lambda: to_left(h, q).wait_send())

    def norm(h):
        step = 16

        @pl.loop(0, T // step)
        def _(i):
            at = pl.ds(pl.multiple_of(i * step, step), step)
            wide = every[h, at, :].astype(jnp.float32)
            square_mean = jnp.mean(wide * wide, axis=1, keepdims=True)
            normed[at, :] = (wide * gain[...] / jnp.sqrt(square_mean + 1e-05)).astype(jnp.bfloat16)

    def expand(hooks):
        tile = 256 if F % 256 == 0 else 128

        @pl.loop(0, F // tile)
        def _(i):
            for k, hook in hooks:
                pl.when(i == min(k, F // tile - 1))(hook)
            at = pl.ds(pl.multiple_of(i * tile, tile), tile)
            gate = jnp.dot(normed[...], gwv[:, at], preferred_element_type=jnp.float32)
            up = jnp.dot(normed[...], uwv[:, at], preferred_element_type=jnp.float32)
            hidden[:, at] = (jax.nn.silu(gate) * up).astype(jnp.bfloat16)

    def reduce(h, hooks):
        @pl.loop(0, n)
        def _(i):
            for k, hook in hooks:
                pl.when(i == min(k, n - 1))(hook)
            q = lax.rem(i, C)
            t = 2 * q + jnp.where(i < C, 1 - c, c)
            at = pl.ds(pl.multiple_of(t * width, width), width)
            part[h, t] = jnp.dot(hidden[...], dwv[:, at], preferred_element_type=jnp.float32).astype(jnp.bfloat16)
            pl.when(i < C)(lambda: to_peer(h, q).start())

    gather_first(0)
    for s in range(1, C):
        gather_step(0, s)
    gather_first(1)
    gather_last(0)
    norm(0)
    loads[0].wait()
    loads[1].wait()
    expand([(4, lambda: gather_step(1, 1))])
    loads[2].wait()
    reduce(0, [(2, lambda: gather_step(1, 2)) if C > 2 else (2, lambda: None)])
    scatter_first(0)
    for s in range(3, C):
        gather_step(1, s)
    gather_last(1)
    norm(1)
    expand([(3, lambda: scatter_step(0, 0))])
    reduce(1, [(2, lambda: scatter_step(0, 1))])
    scatter_first(1)
    for j in range(2, C):
        scatter_step(0, j)
    for j in range(C):
        scatter_step(1, j)
    scatter_last(0)
    scatter_last(1)
    for h in range(H):
        gather_drain(h)
        scatter_drain(h)


def on_device(n, tokens, norm_gain, gate_weight, up_weight, down_weight):
    H = HALVES
    rows, D = tokens.shape
    F = gate_weight.shape[1]
    C = n // 2
    T, width = n * rows // H, D // n
    bf16 = jnp.bfloat16
    any_space, vmem = pl.BlockSpec(memory_space=pl.ANY), pl.BlockSpec(memory_space=pltpu.VMEM)
    dma = pltpu.SemaphoreType.DMA
    return pl.pallas_call(
        functools.partial(block_kernel, n),
        out_shape=jax.ShapeDtypeStruct((n * rows, width), bf16),
        in_specs=[any_space, vmem, any_space, any_space, any_space],
        out_specs=vmem,
        scratch_shapes=[
            pltpu.VMEM((D, F), bf16),
            pltpu.VMEM((D, F), bf16),
            pltpu.VMEM((F, D), bf16),
            pltpu.VMEM((H, T, D), bf16),
            pltpu.VMEM((T, D), bf16),
            pltpu.VMEM((T, F), bf16),
            pltpu.VMEM((H, n, T, width), bf16),
            pltpu.VMEM((H, C, T, width), bf16),
            pltpu.VMEM((H, C + 1, T, width), bf16),
            pltpu.VMEM((T, width), jnp.float32),
            dma((3,)),
            dma((H,)),
            dma((H, n)),
            dma((3, H, n)),
            dma((H, C)),
            dma((H, C)),
            dma((H, C)),
            dma((H, C + 1)),
        ],
        compiler_params=pltpu.CompilerParams(collective_id=0, has_side_effects=True, vmem_limit_bytes=VMEM_LIMIT),
    )(tokens, norm_gain[None, :], gate_weight, up_weight, down_weight)


def solution(mesh):
    return jax.shard_map(
        functools.partial(on_device, mesh.shape["tensor"]),
        mesh=mesh,
        in_specs=(
            P(("dp", "tensor"), None),
            P(),
            P(None, "tensor"),
            P(None, "tensor"),
            P("tensor", None),
        ),
        out_specs=P("dp", "tensor"),
        check_vma=False,
    )
```

time: 212 us -> 101 us (0.48)
  waiting for transfers between devices: 120 us -> 0 us
  Pallas kernels: 0 us -> 98.6 us
  matrix products: 46 us -> 0 us
  blocking collectives: 25.3 us -> 0 us
  between operations: 13.4 us -> 0.01 us
  other arithmetic: 5.41 us -> 0 us
    pallas_call x0 -> x1, Pallas kernels: none -> 98.6 us  [on_device(): pl.pallas_call(functools.partial(block_kernel, n), out_shape=jax.ShapeDty...]
    reduce_scatter x1 -> x0, waiting for transfers between devices: 70.6 us -> none  [on_device(): lax.psum_scatter(jnp.einsum('fc,tf->ct', down_weight, hidden, preferred_e...]
    all_gather x1 -> x0, waiting for transfers between devices: 49.7 us -> none  [on_device(): piece = lax.all_gather(normed, 'tensor', axis=0, tiled=True)]
    dot_general x2 -> x0, matrix products: 46 us -> none  [the longest x1 31.2 us: on_device(): jnp.einsum('fc,tf->ct', down_weight, hidden, preferred_element_type=jnp.f...]
    all_to_all x1 -> x0, blocking collectives: 25.3 us -> none  [on_device(): lax.all_to_all(tokens, 'tensor', split_axis=1, concat_axis=0, tiled=True)]
    convert_element_type x2 -> x0, other arithmetic: 4.16 us -> none  [the longest x1 2.18 us: on_device(): return (residual.astype(jnp.float32) + summed.T).astype(jnp.bfloat16)]
  transfers between devices with their start and end apart: 2 -> 0, of which waited for: 2 -> 0; matrix products, arithmetic and copies ran while one was open for 0% -> 0% of each run, Pallas kernels for 0% -> 0%
where the time goes in v2:
time: 101 us; the launch traced here: 100 us
  Pallas kernels  98.6 us (98%)
  local copies, waits for them, and re-layouts  1.87 us (2%)
    pallas_call x1, Pallas kernels, on_device(): pl.pallas_call(functools.partial(block_kernel, n), out_shape=jax.ShapeDty...  98.6 us

profile of v2, /device:TPU:0, one launch (start us, length us, event | category | flops | bytes accessed | tf_op | source)
XLA Modules:
  0.0 100.5 jit_solution(7771277016268494768)
XLA Ops:
  0.0 98.6 %shard_map.55 = bf16[512,512]{1,0:T(8,128)(2,1)} custom-call(bf16[64,4096]{1,0:T(8,128)(2,1)} %tok.1, f32[1,4096]{1,0:T(1,128)} %bitcast.1, bf16[4096,1792]{1,0:T(8,128)(2,1)} %gw.1, bf16[4096,1792]{1,0:T(8,128)(2,1)} %uw.1, bf16[1792,4096]{1,0:T(8,128)(2,1)} %dw.1), custom_call_target="tpu_custom_call" | custom-call | tf_op jit(solution)/shard_map/pallas_call | solution.py:249
  98.6 1.9 %copy.7 = bf16[512,512]{1,0:T(8,128)(2,1)} copy(bf16[512,512]{1,0:T(8,128)(2,1)} %shard_map.55) | data formatting | bytes 1048576
